TPU v7x, 32 devices: a whole 2x2x4 slice. The times are simulated.
32 devices in a mesh: tm: 4 (over y, x), space: 8 (over z, core).
Axes of the slice: x: 2, y: 2, z: 4, core: 2. Of those that a mesh axis runs over, the one named last changes fastest.
Arguments:
- thermal_field: float32 [128, 49152], P(('tm', 'space')), may hold values from 245 to 255
- seasonal_bucket: int32 [128], replicated, may hold values from 0 to 45, as said below
- season_of_record: int32 [128], replicated, may hold values from 0 to 7
Outputs:
- anomaly: float32 [128, 49152], P(('tm', 'space'))
Inputs may be any that keep to these rules, and one draw needn't show every extreme that they name: `seasonal_bucket`: every group holds at least one day whose year is below 6.
All inputs are finite; a program needn't handle non-finite values.
Results may differ from a plain program's by a relative error of at most 0.0003.
Values sent between devices are 32-bit elements; how exact they have to be, the bound alone decides.
No kernel may reach another device: no remote copies, remote signals or barrier semaphores. Data moves between devices by JAX's collectives and lax.ppermute only.
A program may use at most 64 MiB of HBM per device.

v0:
```python
import jax
import jax.numpy as jnp
from jax import lax
from jax.sharding import PartitionSpec as P

GROUPS = 46
BASE_YEARS = 6


def shards(thermal_field, seasonal_bucket, season_of_record):
    group_ids = jnp.arange(GROUPS, dtype=jnp.int32)
    member = (seasonal_bucket[None, :] == group_ids[:, None]).astype(jnp.float32)
    reference_seasons = member * (season_of_record < BASE_YEARS).astype(jnp.float32)[None, :]
    counts = jnp.sum(reference_seasons, axis=1)
    column_blocks = lax.all_to_all(
        thermal_field, ("tm", "space"), split_axis=1, concat_axis=0, tiled=True
    )
    bucket_aggregates = jnp.dot(
        reference_seasons,
        column_blocks,
        precision=lax.Precision.HIGHEST,
        preferred_element_type=jnp.float32,
    )
    climate = bucket_aggregates / counts[:, None]
    chosen_records = jnp.dot(
        member.T, climate, precision=lax.Precision.HIGHEST, preferred_element_type=jnp.float32
    )
    result = lax.all_to_all(
        column_blocks - chosen_records, ("tm", "space"), split_axis=0, concat_axis=1, tiled=True
    )
    return result


def solution(mesh):
    placed = (P(("tm", "space"), None), P(), P())
    return jax.shard_map(
        shards, mesh=mesh, in_specs=placed, out_specs=P(("tm", "space"), None), check_vma=False
    )
```

profile of v0, /device:TPU:0, one launch (start us, length us, event | category | flops | bytes accessed | tf_op | source)
XLA Modules:
  0.0 55.6 jit_solution(11356422681699996724)
XLA Ops:
  0.0 0.0 copy-start.1
  0.0 7.3 %all-to-all-start = ((f32[4,32,1536]{2,0,1:T(4,128)}), f32[4,32,1536]{2,0,1:T(4,128)S(1)}, u32[]{:S(2)}, u32[]{:S(2)}) async-start(f32[4,32,1536]{2,0,1:T(4,128)} %bitcast.9), calls=%async_computation | async-start | bytes 1572864 | tf_op jit(solution)/shard_map/all_to_all | solution.py:15
  7.3 0.0 copy-done.1
  7.3 0.0 copy-start
  7.4 0.6 %copy-done = s32[128]{0:T(128)S(1)} copy-done((s32[128]{0:T(128)S(1)}, s32[128]{0:T(128)}, u32[]{:S(2)}) %copy-start) | copy-done | bytes 536
  8.0 0.1 select_reduce_fusion
  8.1 21.1 %all-to-all-done = f32[4,32,1536]{2,0,1:T(4,128)S(1)} async-done(((f32[4,32,1536]{2,0,1:T(4,128)}), f32[4,32,1536]{2,0,1:T(4,128)S(1)}, u32[]{:S(2)}, u32[]{:S(2)}) %all-to-all-start) | async-done | bytes 786464 | tf_op jit(solution)/shard_map/all_to_all | solution.py:15
  29.2 0.3 all_to_all.31
  29.5 0.5 convolution_divide_fusion
  30.0 0.5 convolution_subtract_fusion
  30.5 0.2 all_to_all.32
  30.8 24.0 %all_to_all.38 = f32[32,4,1536]{2,1,0:T(4,128)S(1)} all-to-all(f32[32,4,1536]{2,1,0:T(4,128)S(1)} %all_to_all.32), channel_id=1, replica_groups=mesh['tm'=4,'space'=8] {'tm','space'}, dimensions={0} | all-to-all | bytes 1572864 | tf_op jit(solution)/shard_map/all_to_all | solution.py:28
  54.7 0.9 %copy.9 = f32[4,49152]{1,0:T(4,128)} copy(f32[4,49152]{1,0:T(4,128)S(1)} %bitcast.8) | data formatting | bytes 1572864
  (1 shorter events, 0.0 us)
Async XLA Ops:
  0.0 7.3 %copy-start.1 = (s32[128]{0:T(128)S(1)}, s32[128]{0:T(128)}, u32[]{:S(2)}) copy-start(s32[128]{0:T(128)} %param.5) | copy-start | bytes 1540
  0.0 29.2 %all-to-all-start = ((f32[4,32,1536]{2,0,1:T(4,128)}), f32[4,32,1536]{2,0,1:T(4,128)S(1)}, u32[]{:S(2)}, u32[]{:S(2)}) async-start(f32[4,32,1536]{2,0,1:T(4,128)} %bitcast.9), calls=%async_computation | async-start | bytes 1572864 | tf_op jit(solution)/shard_map/all_to_all | solution.py:15
  7.3 0.7 %copy-start = (s32[128]{0:T(128)S(1)}, s32[128]{0:T(128)}, u32[]{:S(2)}) copy-start(s32[128]{0:T(128)} %param.4) | copy-start | bytes 1540
where the time goes:
time: 55.8 us; the launch traced here: 55.6 us
  blocking collectives  24 us (43%)
  waiting for transfers between devices  21.1 us (38%)
  starting transfers between devices  7.33 us (13%)
  local copies, waits for them, and re-layouts  2.02 us (4%)
  matrix products  1.05 us (2%)
    all_to_all x1, blocking collectives, shards(): lax.all_to_all(column_blocks - chosen_records, ('tm', 'space'), split_axi...  24 us
    all_to_all x1, waiting for transfers between devices, shards(): lax.all_to_all(thermal_field, ('tm', 'space'), split_axis=1, concat_axis=...  21.1 us
    all_to_all x1, starting transfers between devices, shards(): lax.all_to_all(thermal_field, ('tm', 'space'), split_axis=1, concat_axis=...  7.33 us
    unnamed x5, local copies, waits for them, and re-layouts  1.52 us
  transfers between devices with their start and end apart: 1, of which 1 were waited for; matrix products, arithmetic and copies ran while one was open for 0% of the time, Pallas kernels for 0%

commit v1 on v0

v1 whole, which is shorter than its diff:
```python
import jax
import jax.numpy as jnp
from jax import lax
from jax.experimental import pallas as pl
from jax.experimental.pallas import tpu as pltpu
from jax.sharding import PartitionSpec as P

BASE_YEARS = 6
AXES = ("tm", "space")
VMEM = pl.BlockSpec(memory_space=pltpu.VMEM)
GRANT = pltpu.CompilerParams(vmem_limit_bytes=32 * 2**20)
SUBLANES = 8


def mates(bucket_ref, season_ref, same_ref, inverse_ref):
    days = bucket_ref.shape[1]
    across = jnp.broadcast_to(bucket_ref[...].astype(jnp.float32), (days, days))
    base = jnp.broadcast_to(season_ref[...], (days, days)) < BASE_YEARS
    same = jnp.where((across.T == across) & base, 1.0, 0.0)
    same_ref[...] = same.astype(jnp.bfloat16)
    counts = jnp.sum(same, axis=1, keepdims=True)
    inverse_ref[...] = jnp.broadcast_to(1.0 / counts, inverse_ref.shape)


def subtract_climate(same_ref, inverse_ref, field_ref, out_ref):
    devices, rows, width = field_ref.shape
    step = max(1, SUBLANES // rows)
    field = jnp.concatenate(
        [
            jnp.concatenate([field_ref[k + j] for j in range(step)], axis=0)
            for k in range(0, devices, step)
        ],
        axis=0,
    )
    high = field.astype(jnp.bfloat16)
    rest = field - high.astype(jnp.float32)
    middle = rest.astype(jnp.bfloat16)
    low = (rest - middle.astype(jnp.float32)).astype(jnp.bfloat16)
    same = same_ref[...]
    sums = jnp.dot(
        jnp.concatenate([same, same, same], axis=1),
        jnp.concatenate([high, middle, low], axis=0),
        preferred_element_type=jnp.float32,
    )
    anomaly = field - sums * inverse_ref[:, :1]
    for k in range(devices):
        out_ref[k] = anomaly[k * rows : (k + 1) * rows]


def shards(thermal_field, seasonal_bucket, season_of_record):
    days = seasonal_bucket.shape[0]
    rows, cells = thermal_field.shape
    devices = days // rows
    width = cells // devices
    same, inverse = pl.pallas_call(
        mates,
        in_specs=[VMEM, VMEM],
        out_specs=(VMEM, VMEM),
        compiler_params=GRANT,
        out_shape=(
            pltpu.VMEM((days, days), jnp.bfloat16),
            pltpu.VMEM((days, 128), jnp.float32),
        ),
    )(seasonal_bucket[None, :], season_of_record[None, :])
    blocks = lax.all_to_all(
        thermal_field.reshape(rows, devices, width), AXES, split_axis=1, concat_axis=0
    )
    anomaly = pl.pallas_call(
        subtract_climate,
        in_specs=[VMEM, VMEM, VMEM],
        out_specs=VMEM,
        compiler_params=GRANT,
        out_shape=pltpu.VMEM((devices, rows, width), jnp.float32),
    )(*(pltpu.with_memory_space_constraint(part, pltpu.VMEM) for part in (same, inverse, blocks)))
    result = lax.all_to_all(anomaly, AXES, split_axis=0, concat_axis=1)
    return result.reshape(rows, cells)


def solution(mesh):
    placed = (P(AXES, None), P(), P())
    return jax.shard_map(
        shards, mesh=mesh, in_specs=placed, out_specs=P(AXES, None), check_vma=False
    )
```

time: 55.8 us -> 54.7 us (0.980)
  matrix products: 1.05 us -> 0 us
  Pallas kernels: 0 us -> 0.58 us
    dot_general x2 -> x0, matrix products: 1.05 us -> none  [the longest x1 0.54 us: shards(): jnp.dot(reference_seasons, column_blocks, precision=lax.Precision.HIGHEST...]
    pallas_call x0 -> x2, Pallas kernels: none -> 0.58 us  [the longest x1 0.41 us: shards(): pl.pallas_call(subtract_climate, in_specs=[VMEM, VMEM, VMEM], out_specs=V...]
where the time goes in v1:
time: 54.7 us; the launch traced here: 54.4 us
  blocking collectives  24 us (44%)
  waiting for transfers between devices  21 us (38%)
  starting transfers between devices  7.33 us (13%)
  local copies, waits for them, and re-layouts  1.54 us (3%)
  Pallas kernels  0.58 us (1%)
    all_to_all x1, blocking collectives, shards(): result = lax.all_to_all(anomaly, AXES, split_axis=0, concat_axis=1)  24 us
    all_to_all x1, waiting for transfers between devices, shards(): lax.all_to_all(thermal_field.reshape(rows, devices, width), AXES, split_a...  21 us
    all_to_all x1, starting transfers between devices, shards(): lax.all_to_all(thermal_field.reshape(rows, devices, width), AXES, split_a...  7.33 us
    unnamed x5, local copies, waits for them, and re-layouts  1.54 us
  transfers between devices with their start and end apart: 1, of which 1 were waited for; matrix products, arithmetic and copies ran while one was open for 0% of the time, Pallas kernels for 0%

profile of v1, /device:TPU:0, one launch (start us, length us, event | category | flops | bytes accessed | tf_op | source)
XLA Modules:
  0.0 54.4 jit_solution(1942369677726611137)
XLA Ops:
  0.0 7.3 %all-to-all-start = ((f32[1,4,32,1536]{3,1,0,2:T(4,128)}), f32[1,4,32,1536]{3,1,0,2:T(4,128)S(1)}, u32[]{:S(2)}, u32[]{:S(2)}) async-start(f32[1,4,32,1536]{3,1,0,2:T(4,128)} %bitcast.21), calls=%async_computation | async-start | bytes 1572864 | tf_op jit(solution)/shard_map/all_to_all | solution.py:65
  7.3 0.0 copy-start
  7.3 0.0 copy-start.1
  7.4 0.6 %copy-done = s32[128]{0:T(128)S(1)} copy-done((s32[128]{0:T(128)S(1)}, s32[128]{0:T(128)}, u32[]{:S(2)}) %copy-start) | copy-done | bytes 536
  8.0 0.0 copy-done.1
  8.0 0.2 shard_map.37
  8.2 21.0 %all-to-all-done = f32[1,4,32,1536]{3,1,0,2:T(4,128)S(1)} async-done(((f32[1,4,32,1536]{3,1,0,2:T(4,128)}), f32[1,4,32,1536]{3,1,0,2:T(4,128)S(1)}, u32[]{:S(2)}, u32[]{:S(2)}) %all-to-all-start) | async-done | bytes 786464 | tf_op jit(solution)/shard_map/all_to_all | solution.py:65
  29.2 0.4 shard_map.38
  29.6 24.0 %all_to_all.30 = f32[32,4,1,1536]{3,1,2,0:T(4,128)S(1)} all-to-all(f32[32,4,1,1536]{3,1,2,0:T(4,128)S(1)} %bitcast.17), channel_id=1, replica_groups=mesh['tm'=4,'space'=8] {'tm','space'}, dimensions={0} | all-to-all | bytes 1572864 | tf_op jit(solution)/shard_map/all_to_all | solution.py:75
  53.6 0.9 %copy.6 = f32[4,49152]{1,0:T(4,128)} copy(f32[4,49152]{1,0:T(4,128)S(1)} %bitcast.20) | data formatting | bytes 1572864
Async XLA Ops:
  0.0 29.2 %all-to-all-start = ((f32[1,4,32,1536]{3,1,0,2:T(4,128)}), f32[1,4,32,1536]{3,1,0,2:T(4,128)S(1)}, u32[]{:S(2)}, u32[]{:S(2)}) async-start(f32[1,4,32,1536]{3,1,0,2:T(4,128)} %bitcast.21), calls=%async_computation | async-start | bytes 1572864 | tf_op jit(solution)/shard_map/all_to_all | solution.py:65
  7.3 0.7 %copy-start = (s32[128]{0:T(128)S(1)}, s32[128]{0:T(128)}, u32[]{:S(2)}) copy-start(s32[128]{0:T(128)} %param.4) | copy-start | bytes 1540
  7.3 0.7 %copy-start.1 = (s32[128]{0:T(128)S(1)}, s32[128]{0:T(128)}, u32[]{:S(2)}) copy-start(s32[128]{0:T(128)} %param.5) | copy-start | bytes 1540

commit v2 on v1

--- a/solution.py
+++ b/solution.py
@@ -1,5 +1,8 @@
+import random
+
 import jax
 import jax.numpy as jnp
+import numpy as np
 from jax import lax
 from jax.experimental import pallas as pl
 from jax.experimental.pallas import tpu as pltpu
@@ -47,11 +50,22 @@
         out_ref[k] = anomaly[k * rows : (k + 1) * rows]
 
 
+def ranks(devices):
+    order = list(range(devices))
+    random.Random(1).shuffle(order)
+    return order
+
+
 def shards(thermal_field, seasonal_bucket, season_of_record):
     days = seasonal_bucket.shape[0]
     rows, cells = thermal_field.shape
     devices = days // rows
     width = cells // devices
+    order = ranks(devices)
+    bucket, season = (
+        jnp.take(days_of, np.asarray(order), axis=0).reshape(1, days)
+        for days_of in (seasonal_bucket.reshape(devices, rows), season_of_record.reshape(devices, rows))
+    )
     same, inverse = pl.pallas_call(
         mates,
         in_specs=[VMEM, VMEM],
@@ -61,9 +75,10 @@
             pltpu.VMEM((days, days), jnp.bfloat16),
             pltpu.VMEM((days, 128), jnp.float32),
         ),
-    )(seasonal_bucket[None, :], season_of_record[None, :])
+    )(bucket, season)
     blocks = lax.all_to_all(
-        thermal_field.reshape(rows, devices, width), AXES, split_axis=1, concat_axis=0
+        thermal_field.reshape(rows, devices, width), AXES, split_axis=1, concat_axis=0,
+        axis_index_groups=[order],
     )
     anomaly = pl.pallas_call(
         subtract_climate,
@@ -72,7 +87,9 @@
         compiler_params=GRANT,
         out_shape=pltpu.VMEM((devices, rows, width), jnp.float32),
     )(*(pltpu.with_memory_space_constraint(part, pltpu.VMEM) for part in (same, inverse, blocks)))
-    result = lax.all_to_all(anomaly, AXES, split_axis=0, concat_axis=1)
+    result = lax.all_to_all(
+        anomaly, AXES, split_axis=0, concat_axis=1, axis_index_groups=[order]
+    )
     return result.reshape(rows, cells)
 
 

time: 54.7 us -> 52.4 us (0.958)
  waiting for transfers between devices: 21 us -> 17.2 us
  local copies, waits for them, and re-layouts: 1.54 us -> 3.52 us
  blocking collectives: 24 us -> 23.4 us
    all_to_all x1, waiting for transfers between devices: 21 us -> 17.2 us  [shards(): lax.all_to_all(thermal_field.reshape(rows, devices, width), AXES, split_a...]
    gather x0 -> x2, local copies, waits for them, and re-layouts: none -> 1.15 us  [shards(): jnp.take(days_of, np.asarray(order), axis=0).reshape(1, days)]
    unnamed x5 -> x7, local copies, waits for them, and re-layouts: 1.54 us -> 1.98 us
  transfers between devices with their start and end apart: 1 -> 1, of which waited for: 1 -> 1; matrix products, arithmetic and copies ran while one was open for 0% -> 3% of each run, Pallas kernels for 0% -> 0%
where the time goes in v2:
time: 52.4 us; the launch traced here: 52.1 us
  blocking collectives  23.4 us (45%)
  waiting for transfers between devices  17.2 us (33%)
  starting transfers between devices  7.33 us (14%)
  local copies, waits for them, and re-layouts  3.52 us (7%)
  Pallas kernels  0.59 us (1%)
    all_to_all x1, blocking collectives, shards(): lax.all_to_all(anomaly, AXES, split_axis=0, concat_axis=1, axis_index_gro...  23.4 us
    all_to_all x1, waiting for transfers between devices, shards(): lax.all_to_all(thermal_field.reshape(rows, devices, width), AXES, split_a...  17.2 us
    all_to_all x1, starting transfers between devices, shards(): lax.all_to_all(thermal_field.reshape(rows, devices, width), AXES, split_a...  7.33 us
    unnamed x7, local copies, waits for them, and re-layouts  1.98 us
    gather x2, local copies, waits for them, and re-layouts, shards(): jnp.take(days_of, np.asarray(order), axis=0).reshape(1, days)  1.15 us
  transfers between devices with their start and end apart: 1, of which 1 were waited for; matrix products, arithmetic and copies ran while one was open for 3% of the time, Pallas kernels for 0%

profile of v2, /device:TPU:0, one launch (start us, length us, event | category | flops | bytes accessed | tf_op | source)
XLA Modules:
  0.0 52.1 jit_solution(11240038651010793310)
XLA Ops:
  0.0 0.0 copy-start
  0.0 7.3 %all-to-all-start = ((f32[1,4,32,1536]{3,1,0,2:T(4,128)}), f32[1,4,32,1536]{3,1,0,2:T(4,128)S(1)}, u32[]{:S(2)}, u32[]{:S(2)}) async-start(f32[1,4,32,1536]{3,1,0,2:T(4,128)} %bitcast.17), calls=%async_computation | async-start | bytes 1572864 | tf_op jit(solution)/shard_map/all_to_all | solution.py:79
  7.3 0.0 copy-done
  7.3 0.0 copy-start.2
  7.4 0.1 reshape.19
  7.5 0.5 %copy-done.2 = s32[32]{0:T(128)S(1)} copy-done((s32[32]{0:T(128)S(1)}, s32[32]{0:T(128)}, u32[]{:S(2)}) %copy-start.2) | copy-done | bytes 152
  8.0 0.6 %gather_fusion = s32[32,4]{1,0:T(8,128)S(1)} fusion(s32[32,4]{1,0:T(8,128)S(1)} %reshape.19, s32[1024]{0:T(1024)S(1)} %pad_clamp_fusion), kind=kCustom, calls=%fused_computation.clone | custom fusion | bytes 1152 | tf_op jit(solution)/shard_map/jit(_take)/gather | solution.py:66
  8.6 0.0 copy-start.1
  8.6 0.1 reshape.20.bucket_ref
  8.7 0.5 %copy-done.1 = s32[128]{0:T(128)S(1)} copy-done((s32[128]{0:T(128)S(1)}, s32[128]{0:T(128)}, u32[]{:S(2)}) %copy-start.1) | copy-done | bytes 536
  9.2 0.1 reshape.21
  9.3 0.6 %gather_fusion.1 = s32[32,4]{1,0:T(8,128)S(1)} fusion(s32[32,4]{1,0:T(8,128)S(1)} %reshape.21, s32[1024]{0:T(1024)S(1)} %pad_clamp_fusion), kind=kCustom, calls=%fused_computation.1.clone | custom fusion | bytes 1152 | tf_op jit(solution)/shard_map/jit(_take)/gather | solution.py:66
  9.9 0.1 reshape.22.season_ref
  10.0 0.2 shard_map.55
  10.2 17.2 %all-to-all-done = f32[1,4,32,1536]{3,1,0,2:T(4,128)S(1)} async-done(((f32[1,4,32,1536]{3,1,0,2:T(4,128)}), f32[1,4,32,1536]{3,1,0,2:T(4,128)S(1)}, u32[]{:S(2)}, u32[]{:S(2)}) %all-to-all-start) | async-done | bytes 786464 | tf_op jit(solution)/shard_map/all_to_all | solution.py:79
  27.4 0.4 shard_map.56
  27.8 23.4 %all_to_all.30 = f32[32,4,1,1536]{3,1,2,0:T(4,128)S(1)} all-to-all(f32[32,4,1,1536]{3,1,2,0:T(4,128)S(1)} %bitcast.15), channel_id=1, replica_groups={{26,17,11,10,28,1,5,4,7,16,9,19,30,13,22,0,21,29,6,12,20,23,14,15,3,31,..., dimensions={0} | all-to-all | bytes 1572864 | tf_op jit(solution)/shard_map/all_to_all | solution.py:90
  51.2 0.9 %copy.8 = f32[4,49152]{1,0:T(4,128)} copy(f32[4,49152]{1,0:T(4,128)S(1)} %bitcast.16) | data formatting | bytes 1572864
  (1 shorter events, 0.0 us)
Async XLA Ops:
  0.0 7.3 %copy-start = (s32[128]{0:T(128)S(1)}, s32[128]{0:T(128)}, u32[]{:S(2)}) copy-start(s32[128]{0:T(128)} %param.8) | copy-start | bytes 1540
  0.0 27.4 %all-to-all-start = ((f32[1,4,32,1536]{3,1,0,2:T(4,128)}), f32[1,4,32,1536]{3,1,0,2:T(4,128)S(1)}, u32[]{:S(2)}, u32[]{:S(2)}) async-start(f32[1,4,32,1536]{3,1,0,2:T(4,128)} %bitcast.17), calls=%async_computation | async-start | bytes 1572864 | tf_op jit(solution)/shard_map/all_to_all | solution.py:79
  7.3 0.7 %copy-start.2 = (s32[32]{0:T(128)S(1)}, s32[32]{0:T(128)}, u32[]{:S(2)}) copy-start(s32[32]{0:T(128)} %constant.32) | copy-start | bytes 388
  8.6 0.7 %copy-start.1 = (s32[128]{0:T(128)S(1)}, s32[128]{0:T(128)}, u32[]{:S(2)}) copy-start(s32[128]{0:T(128)} %param.9) | copy-start | bytes 1540
